TPU v7x, 256 devices: a 4x2x16 block of a 4x16x16 slice. The times are simulated.
256 devices in a mesh: scan: 2 (over y), slab: 128 (over z, x, core).
Axes of the slice: x: 4, y: 2, z: 16, core: 2. Of those that a mesh axis runs over, the one named last changes fastest.
The devices are a block of a 4x16x16 slice.
Arguments:
- image: float32 [2, 128, 256, 128], P(None, 'slab', 'scan'), parts along dimension 2, may hold values from -6 to 6
- sensitivity: bfloat16 [12, 2, 128, 128, 128], P('scan', None, 'slab'), parts along dimension 0, may hold values from -1.5 to 1.5
- kernel: float32 [256, 256, 256], P(None, 'slab'), may hold values from 0.1 to 4
Outputs:
- normal_image: float32 [2, 128, 256, 128], P(None, 'slab', 'scan'), parts along dimension 2
There are 2 independent parts, one for each index of `scan`. A program takes and returns all parts, laid end to end along the dimension named above; an argument that names none is the same for every part. Nothing has to cross between parts.
All inputs are finite; a program needn't handle non-finite values.
Results may differ from a plain program's by a relative error of at most 0.0024.
Values may be sent and summed in bfloat16 or wider, within the bound.
A program may use at most 64 MiB of HBM per device.

v0:
```python
import math

import jax
import jax.numpy as jnp
from jax import lax
from jax.sharding import PartitionSpec as P

NX = 128
NY = 128
NZ = 128
GX = 256
GY = 256
GZ = 256


smooth_weight = 0.1


def with_halo(cells, sides, width):
    for axis, dim in sides:
        count = lax.axis_size(axis)
        ends = count - 1
        head = lax.slice_in_dim(cells, 0, width, axis=dim)
        tail = lax.slice_in_dim(cells, cells.shape[dim] - width, cells.shape[dim], axis=dim)
        cells = jnp.concatenate(
            [
                lax.ppermute(tail, axis, [(i, (i + 1) % count) for i in range(ends)]),
                cells,
                lax.ppermute(head, axis, [((i + 1) % count, i) for i in range(ends)]),
            ],
            axis=dim,
        )
    return cells


def fourier_table(count_out, count_in, length, sign_value):
    row_index = lax.broadcasted_iota(jnp.int32, (count_out, count_in), 0)
    column_index = lax.broadcasted_iota(jnp.int32, (count_out, count_in), 1)
    phases = row_index * column_index % length
    angles = phases.astype(jnp.float32) * (2.0 * math.pi / length)
    factor = 1.0 / math.sqrt(length)
    real_part = jnp.cos(angles) * factor
    imaginary = sign_value * jnp.sin(angles) * factor
    stacked = jnp.stack([jnp.stack([real_part, -imaginary]), jnp.stack([imaginary, real_part])])
    return stacked.astype(jnp.bfloat16)


def apply_table(matrix, values, pattern):
    return jnp.einsum(pattern, matrix, values, preferred_element_type=jnp.float32)


def local(image, sensitivity, kernel):
    forward_first = fourier_table(GX, NX, GX, -1.0)
    forward_second = fourier_table(GY, NY, GY, -1.0)
    forward_third = fourier_table(GZ, NZ, GZ, -1.0)
    inverse_first = fourier_table(NX, GX, GX, 1.0)
    inverse_second = fourier_table(NY, GY, GY, 1.0)
    inverse_third = fourier_table(NZ, GZ, GZ, 1.0)
    coil_real = sensitivity[:, 0].astype(jnp.float32)
    coil_imaginary = sensitivity[:, 1].astype(jnp.float32)
    coil_images = jnp.stack(
        [
            coil_real * image[0] - coil_imaginary * image[1],
            coil_real * image[1] + coil_imaginary * image[0],
        ],
        axis=1,
    ).astype(jnp.bfloat16)
    along_second = apply_table(forward_second, coil_images, "pqkj,cqajb->cpakb").astype(
        jnp.bfloat16
    )
    along_third = apply_table(
        forward_third,
        lax.all_to_all(along_second, "slab", split_axis=3, concat_axis=2, tiled=True),
        "pqkj,cqabj->cpabk",
    ).astype(jnp.bfloat16)
    spectrum = apply_table(forward_first, along_third, "pqkj,cqjab->cpkab")
    filtered = (spectrum * kernel).astype(jnp.bfloat16)
    back_first = apply_table(inverse_first, filtered, "pqkj,cqjab->cpkab").astype(jnp.bfloat16)
    back_third = apply_table(inverse_third, back_first, "pqkj,cqabj->cpabk").astype(jnp.bfloat16)
    back_third = lax.all_to_all(back_third, "slab", split_axis=2, concat_axis=3, tiled=True)
    coil_results = apply_table(inverse_second, back_third, "pqkj,cqajb->cpakb")
    summed_real = jnp.sum(
        coil_real * coil_results[:, 0] + coil_imaginary * coil_results[:, 1], axis=0
    )
    summed_imaginary = jnp.sum(
        coil_real * coil_results[:, 1] - coil_imaginary * coil_results[:, 0], axis=0
    )
    padded = with_halo(image.astype(jnp.bfloat16), (("slab", 1),), 1).astype(image.dtype)
    beside = padded[:, 2:] + padded[:, :-2]
    local_pad = jnp.pad(image, ((0, 0), (0, 0), (1, 1), (1, 1)))
    beside = beside + local_pad[:, :, 2:, 1:-1] + local_pad[:, :, :-2, 1:-1]
    beside = beside + local_pad[:, :, 1:-1, 2:] + local_pad[:, :, 1:-1, :-2]
    penalty = 6.0 * image - beside
    return jnp.stack([summed_real, summed_imaginary]) + smooth_weight * penalty


def solution(mesh):
    return jax.shard_map(
        local,
        mesh=mesh,
        in_specs=(
            P(None, "slab", "scan", None),
            P("scan", None, "slab", None, None),
            P(None, "slab", None),
        ),
        out_specs=P(None, "slab", "scan", None),
        check_vma=False,
    )
```

profile of v0, /device:TPU:33, one launch (start us, length us, event | category | flops | bytes accessed | tf_op | source)
XLA Modules:
  0.0 139.0 jit_solution(14245791856360535516)
XLA Ops:
  0.0 0.5 negate_convert_fusion.1
  0.6 0.5 fusion.58
  1.1 1.1 fusion.66
  2.1 0.2 copy.65
  2.3 0.2 copy.66
  2.5 0.1 copy.22
  2.6 0.1 copy.24
  2.7 0.1 fusion.38
  2.9 0.4 fusion.15
  3.3 0.0 copy-start
  3.3 1.9 %copy.26 = bf16[6,2,1,256,128]{4,1,0,2,3:T(2,128)(2,1)} copy(bf16[6,2,1,256,128]{3,4,1,0,2:T(8,128)(2,1)S(1)} %fusion.15) | data formatting | bytes 1572864 | tf_op jit(solution)/shard_map/convert_element_type | solution.py:68
  5.2 31.0 %all-to-all-start = ((bf16[6,2,1,256,128]{4,1,0,2,3:T(2,128)(2,1)}), bf16[6,2,1,256,128]{4,1,0,2,3:T(2,128)(2,1)S(1)}, u32[]{:S(2)}, u32[]{:S(2)}) async-start(bf16[6,2,1,256,128]{4,1,0,2,3:T(2,128)(2,1)} %copy.26), calls=%async_computation | async-start | bytes 1572864 | tf_op jit(solution)/shard_map/all_to_all | solution.py:73
  36.2 1.0 copy.30
  37.2 0.5 fusion.59
  37.7 0.5 negate_convert_fusion
  38.3 38.4 %all-to-all-done = bf16[6,2,1,256,128]{4,1,0,2,3:T(2,128)(2,1)S(1)} async-done(((bf16[6,2,1,256,128]{4,1,0,2,3:T(2,128)(2,1)}), bf16[6,2,1,256,128]{4,1,0,2,3:T(2,128)(2,1)S(1)}, u32[]{:S(2)}, u32[]{:S(2)}) %all-to-all-start) | async-done | bytes 786464 | tf_op jit(solution)/shard_map/all_to_all | solution.py:73
  76.7 0.6 bitcast_convert_fusion.1
  77.3 4.1 %bitcast_convert_fusion = bf16[6,2,256,2,128]{4,2,3,1,0:T(8,128)(2,1)} fusion(f32[256,2,256]{0,2,1:T(8,128)} %copy.30, bf16[6,128,2,2,256]{4,1,3,2,0:T(8,128)(2,1)S(1)} %bitcast_convert_fusion.1, bf16[1,2,128,256]{3,2,1,0:T(8,128)(2,1)S(1)} %get-tuple-element.14, bf16[1,2,128,256]{3,2,1,0:T(8,128)(2,1)S(1)} %get-tuple-element.13, ...), kind=kOutput, calls=%fused_computation.4 | convolution fusion | flops 1615593472 | bytes 4194304 | tf_op jit(solution)/shard_map/pqkj,cqjab->cpkab/dot_general | solution.py:49
  81.4 2.0 %fusion.16 = bf16[6,2,128,2,128]{4,2,1,3,0:T(8,128)(2,1)S(1)} fusion(bf16[6,2,256,2,128]{4,2,3,1,0:T(8,128)(2,1)} %bitcast_convert_fusion, bf16[1,2,128,256]{3,2,1,0:T(8,128)(2,1)S(1)} %get-tuple-element.14, bf16[1,2,128,256]{3,2,1,0:T(8,128)(2,1)S(1)} %get-tuple-element.13), kind=kOutput, calls=%fused_computation.15 | convolution fusion | flops 403570688 | bytes 2621440 | tf_op jit(solution)/shard_map/pqkj,cqabj->cpabk/dot_general | solution.py:49
  83.5 1.7 %copy.32 = bf16[6,2,128,2,128]{4,1,3,0,2:T(2,128)(2,1)} copy(bf16[6,2,128,2,128]{4,2,1,3,0:T(8,128)(2,1)S(1)} %fusion.16) | data formatting | bytes 1572864 | tf_op jit(solution)/shard_map/convert_element_type | solution.py:79
  85.1 11.4 %all-to-all-start.1 = ((bf16[6,2,128,2,128]{4,1,3,0,2:T(2,128)(2,1)}), bf16[6,2,128,2,128]{4,1,3,0,2:T(2,128)(2,1)S(1)}, u32[]{:S(2)}, u32[]{:S(2)}) async-start(bf16[6,2,128,2,128]{4,1,3,0,2:T(2,128)(2,1)} %copy.32), calls=%async_computation.1 | async-start | bytes 1572864 | tf_op jit(solution)/shard_map/all_to_all | solution.py:80
  96.5 0.1 copy.36
  96.7 3.6 %collective-permute-start = (bf16[2,1,128,128]{2,3,1,0:T(8,128)(2,1)S(1)}, bf16[2,1,128,128]{2,3,1,0:T(8,128)(2,1)S(1)}, u32[]{:S(2)}, u32[]{:S(2)}) collective-permute-start(bf16[2,1,128,128]{2,3,1,0:T(8,128)(2,1)S(1)} %convert_element_type.154), channel_id=1, source_target_pairs={{0,1},{1,2},{2,3},{3,4},{4,5},{5,6},{6,7},{7,8},{8,9},{9,10},{10,1... | collective-permute-start | bytes 196616 | tf_op jit(solution)/shard_map/ppermute | solution.py:27
  100.2 2.3 %collective-permute-start.1 = (bf16[2,1,128,128]{2,3,1,0:T(8,128)(2,1)S(1)}, bf16[2,1,128,128]{2,3,1,0:T(8,128)(2,1)S(1)}, u32[]{:S(2)}, u32[]{:S(2)}) collective-permute-start(bf16[2,1,128,128]{2,3,1,0:T(8,128)(2,1)S(1)} %convert_element_type.154), channel_id=1, source_target_pairs={{1,0},{2,1},{3,2},{4,3},{5,4},{6,5},{7,6},{8,7},{9,8},{10,9},{11,1... | collective-permute-start | bytes 196616 | tf_op jit(solution)/shard_map/ppermute | solution.py:29
  102.5 34.5 %all-to-all-done.1 = bf16[6,2,128,2,128]{4,1,3,0,2:T(2,128)(2,1)S(1)} async-done(((bf16[6,2,128,2,128]{4,1,3,0,2:T(2,128)(2,1)}), bf16[6,2,128,2,128]{4,1,3,0,2:T(2,128)(2,1)S(1)}, u32[]{:S(2)}, u32[]{:S(2)}) %all-to-all-start.1) | async-done | bytes 786464 | tf_op jit(solution)/shard_map/all_to_all | solution.py:80
  137.0 0.5 copy.33
  137.5 0.4 convolution_bitcast_fusion
  138.0 0.1 fusion.25
  138.1 0.0 collective-permute-done
  138.1 0.0 collective-permute-done.1
  138.1 0.1 fusion.51
  138.3 0.8 copy.39
  (7 shorter events, 0.1 us)
Async XLA Ops:
  0.0 2.5 %copy-start.1 = (f32[2,1,128,128]{3,2,1,0:T(8,128)S(1)}, f32[2,1,128,128]{3,2,1,0:T(8,128)}, u32[]{:S(2)}) copy-start(f32[2,1,128,128]{3,2,1,0:T(8,128)} %param.3) | copy-start | bytes 393220
  3.3 32.9 %copy-start = (f32[256,2,256]{2,1,0:T(2,128)S(1)}, f32[256,2,256]{2,1,0:T(2,128)}, u32[]{:S(2)}) copy-start(f32[256,2,256]{2,1,0:T(2,128)} %param.5) | copy-start | bytes 1572868
  5.2 71.5 %all-to-all-start = ((bf16[6,2,1,256,128]{4,1,0,2,3:T(2,128)(2,1)}), bf16[6,2,1,256,128]{4,1,0,2,3:T(2,128)(2,1)S(1)}, u32[]{:S(2)}, u32[]{:S(2)}) async-start(bf16[6,2,1,256,128]{4,1,0,2,3:T(2,128)(2,1)} %copy.26), calls=%async_computation | async-start | bytes 1572864 | tf_op jit(solution)/shard_map/all_to_all | solution.py:73
  85.1 51.9 %all-to-all-start.1 = ((bf16[6,2,128,2,128]{4,1,3,0,2:T(2,128)(2,1)}), bf16[6,2,128,2,128]{4,1,3,0,2:T(2,128)(2,1)S(1)}, u32[]{:S(2)}, u32[]{:S(2)}) async-start(bf16[6,2,128,2,128]{4,1,3,0,2:T(2,128)(2,1)} %copy.32), calls=%async_computation.1 | async-start | bytes 1572864 | tf_op jit(solution)/shard_map/all_to_all | solution.py:80
  96.7 41.4 %collective-permute-start = (bf16[2,1,128,128]{2,3,1,0:T(8,128)(2,1)S(1)}, bf16[2,1,128,128]{2,3,1,0:T(8,128)(2,1)S(1)}, u32[]{:S(2)}, u32[]{:S(2)}) collective-permute-start(bf16[2,1,128,128]{2,3,1,0:T(8,128)(2,1)S(1)} %convert_element_type.154), channel_id=1, source_target_pairs={{0,1},{1,2},{2,3},{3,4},{4,5},{5,6},{6,7},{7,8},{8,9},{9,10},{10,1... | collective-permute-start | bytes 196616 | tf_op jit(solution)/shard_map/ppermute | solution.py:27
  100.2 37.9 %collective-permute-start.1 = (bf16[2,1,128,128]{2,3,1,0:T(8,128)(2,1)S(1)}, bf16[2,1,128,128]{2,3,1,0:T(8,128)(2,1)S(1)}, u32[]{:S(2)}, u32[]{:S(2)}) collective-permute-start(bf16[2,1,128,128]{2,3,1,0:T(8,128)(2,1)S(1)} %convert_element_type.154), channel_id=1, source_target_pairs={{1,0},{2,1},{3,2},{4,3},{5,4},{6,5},{7,6},{8,7},{9,8},{10,9},{11,1... | collective-permute-start | bytes 196616 | tf_op jit(solution)/shard_map/ppermute | solution.py:29
where the time goes:
time: 141 us; the launch traced here: 139 us
  waiting for transfers between devices  72.9 us (52%)
  starting transfers between devices  48.2 us (34%)
  matrix products  7.59 us (5%)
  local copies, waits for them, and re-layouts  7.55 us (5%)
  other arithmetic  2.58 us (2%)
    all_to_all x1, waiting for transfers between devices, local(): lax.all_to_all(along_second, 'slab', split_axis=3, concat_axis=2, tiled=T...  38.4 us
    all_to_all x1, waiting for transfers between devices, local(): lax.all_to_all(back_third, 'slab', split_axis=2, concat_axis=3, tiled=True)  34.5 us
    all_to_all x1, starting transfers between devices, local(): lax.all_to_all(along_second, 'slab', split_axis=3, concat_axis=2, tiled=T...  31 us
    all_to_all x1, starting transfers between devices, local(): lax.all_to_all(back_third, 'slab', split_axis=2, concat_axis=3, tiled=True)  11.4 us
    dot_general x5, matrix products, apply_table(): jnp.einsum(pattern, matrix, values, preferred_element_type=jnp.float32)  7.59 us
    ppermute x1, starting transfers between devices, with_halo(): lax.ppermute(tail, axis, [(i, (i + 1) % count) for i in range(ends)])  3.57 us
  transfers between devices with their start and end apart: 4, of which 2 were waited for; matrix products, arithmetic and copies ran while one was open for 2% of the time, Pallas kernels for 0%

commit v1 on v0

v1 whole, which is shorter than its diff:
```python
import functools
import math

import jax
import jax.numpy as jnp
import ml_dtypes
import numpy as np
from jax import lax
from jax.experimental import pallas as pl
from jax.experimental.pallas import tpu as pltpu
from jax.sharding import PartitionSpec as P

MESH = pl.DeviceIdType.MESH
smooth_weight = 0.1


def factor(count_out, count_in, length, sign):
    phases = np.outer(np.arange(count_out), np.arange(count_in)) % length
    angles = phases.astype(np.float32) * np.float32(2.0 * math.pi / length)
    scale = np.float32(1.0 / math.sqrt(length))
    return np.cos(angles) * scale, sign * np.sin(angles) * scale


def stacked(real, imaginary):
    rows = np.stack([np.stack([real, -imaginary], 1), np.stack([imaginary, real], 1)])
    return rows.astype(ml_dtypes.bfloat16)


def tables(nx, ny, nz, gx, gy, gz):
    fx, fy, fz = (stacked(*factor(g, n, g, -1.0)) for n, g in ((nx, gx), (ny, gy), (nz, gz)))
    hx, hy, hz = (stacked(*factor(n, g, g, 1.0)) for n, g in ((nx, gx), (ny, gy), (nz, gz)))
    return (
        fy.transpose(1, 0, 2, 3).reshape(2 * gy, 2 * ny),
        fx.transpose(0, 1, 3, 2).reshape(2 * gx, 2 * nx),
        fz.transpose(2, 3, 0, 1).reshape(2 * nz, 2 * gz),
        hz.transpose(2, 3, 0, 1).reshape(2 * gz, 2 * nz),
        hx.transpose(1, 0, 2, 3).reshape(2 * nx, 2 * gx),
        hy.transpose(0, 1, 3, 2).reshape(2 * ny, 2 * gy),
    )


def dot(a, b):
    return jnp.dot(a, b, preferred_element_type=jnp.float32)


def body(
    n,
    image_hbm,
    maps_hbm,
    kernel_hbm,
    *refs,
):
    table_hbm, refs = refs[:6], refs[6:]
    (out, image, maps, weight, *refs) = refs
    table, refs = refs[:6], refs[6:]
    (lines, spectra, backs, planes, face, halo, total, load_sem, out_sem, in_sem, back_out_sem, back_in_sem, face_sem, halo_sem) = refs
    coils, _, ny, nz = maps.shape
    per = lines.shape[2]
    me = lax.axis_index("slab")

    loads = [pltpu.make_async_copy(image_hbm.at[:, 0], image, load_sem.at[0])]
    loads.append(pltpu.make_async_copy(maps_hbm.at[:, :, 0], maps, load_sem.at[1]))
    for i in range(6):
        loads.append(pltpu.make_async_copy(table_hbm[i], table[i], load_sem.at[2 + i]))
    for i in range(per):
        loads.append(pltpu.make_async_copy(kernel_hbm.at[:, i], weight.at[i], load_sem.at[8 + i]))
    for load in loads:
        load.start()

    barrier = pltpu.get_barrier_semaphore()

    def greet(k, carry):
        pl.semaphore_signal(
            barrier, inc=1, device_id={"slab": lax.rem(me + k, n)}, device_id_type=MESH
        )
        return carry

    lax.fori_loop(1, n, greet, 0)

    for load in loads[:3]:
        load.wait()
    face[...] = image[...].astype(face.dtype)

    def spread(c, carry):
        real, imaginary = maps[c, 0].astype(jnp.float32), maps[c, 1].astype(jnp.float32)
        coil_real = real * image[0] - imaginary * image[1]
        coil_imaginary = real * image[1] + imaginary * image[0]
        coil = jnp.concatenate([coil_real, coil_imaginary]).astype(jnp.bfloat16)
        along = dot(table[0][...], coil).astype(jnp.bfloat16)
        lines.at[c].reshape(n * per * 2, nz)[...] = along
        spectra[c, :, me] = lines[c, me]
        return carry

    lax.fori_loop(0, coils, spread, 0)
    pl.semaphore_wait(barrier, n - 1)

    def send(c, d):
        pltpu.make_async_remote_copy(
            lines.at[c, d],
            spectra.at[c, :, me],
            out_sem.at[c],
            in_sem.at[c],
            device_id={"slab": d},
            device_id_type=MESH,
        ).start()

    def send_back(c, d):
        pltpu.make_async_remote_copy(
            backs.at[c, :, d],
            planes.at[c, me],
            back_out_sem.at[c],
            back_in_sem.at[c],
            device_id={"slab": d},
            device_id_type=MESH,
        ).start()

    def each(act, c):
        def step(k, carry):
            act(c, lax.rem(me + k, n))
            return carry

        lax.fori_loop(1, n, step, 0)

    def face_copy(side):
        return pltpu.make_async_remote_copy(
            face,
            halo.at[side],
            face_sem.at[side],
            halo_sem.at[side],
            device_id={"slab": lax.rem(me + (1 if side == 0 else n - 1), n)},
            device_id_type=MESH,
        )

    @pl.when(me < n - 1)
    def _():
        face_copy(0).start()

    @pl.when(me > 0)
    def _():
        face_copy(1).start()

    def start(c, carry):
        each(send, c)
        return carry

    lax.fori_loop(0, coils, start, 0)
    for load in loads[3:]:
        load.wait()

    def middle(c, carry):
        arrived = spectra.at[c, :, pl.ds(0, n - 1)]
        pltpu.make_async_copy(arrived, arrived, in_sem.at[c]).wait()
        for i in range(per):
            x = spectra.at[c, i].reshape(2 * n, nz)[...]
            along = dot(table[1][...], x).astype(jnp.bfloat16)
            half = along.shape[0] // 2
            rows = jnp.concatenate([along[:half], along[half:]], axis=1)
            spectrum = dot(rows, table[2][...])
            gz = spectrum.shape[1] // 2
            k = weight[i]
            filtered = jnp.concatenate(
                [spectrum[:, :gz] * k, spectrum[:, gz:] * k], axis=1
            ).astype(jnp.bfloat16)
            back = dot(filtered, table[3][...]).astype(jnp.bfloat16)
            columns = jnp.concatenate([back[:, :nz], back[:, nz:]], axis=0)
            first = dot(table[4][...], columns).astype(jnp.bfloat16)
            backs.at[c, i].reshape(2 * n, nz)[...] = first
        planes[c, me] = backs[c, :, me]
        each(send_back, c)
        return carry

    lax.fori_loop(0, coils, middle, 0)

    @pl.when(me > 0)
    def _():
        face_copy(0).wait_recv()

    @pl.when(me == 0)
    def _():
        halo[0] = jnp.zeros_like(halo[0])

    @pl.when(me < n - 1)
    def _():
        face_copy(1).wait_recv()

    @pl.when(me == n - 1)
    def _():
        halo[1] = jnp.zeros_like(halo[1])

    for p in range(2):
        plane = image[p]
        beside = halo[0, p].astype(jnp.float32) + halo[1, p].astype(jnp.float32)
        row, column = jnp.zeros((1, nz), jnp.float32), jnp.zeros((ny, 1), jnp.float32)
        beside += jnp.concatenate([plane[1:], row], axis=0) + jnp.concatenate([row, plane[:-1]], axis=0)
        beside += jnp.concatenate([plane[:, 1:], column], axis=1) + jnp.concatenate([column, plane[:, :-1]], axis=1)
        total[p] = smooth_weight * (6.0 * plane - beside)

    def finish(c, carry):
        arrived = planes.at[c, pl.ds(0, n - 1)]
        pltpu.make_async_copy(arrived, arrived, back_in_sem.at[c]).wait()
        coil = dot(table[5][...], planes.at[c].reshape(n * per * 2, nz)[...])
        coil_real, coil_imaginary = coil[:ny], coil[ny:]
        real, imaginary = maps[c, 0].astype(jnp.float32), maps[c, 1].astype(jnp.float32)
        total[0] += real * coil_real + imaginary * coil_imaginary
        total[1] += real * coil_imaginary - imaginary * coil_real
        return carry

    lax.fori_loop(0, coils, finish, 0)
    out[:, 0] = total[...]

    def drain(c, carry):
        left = lines.at[c, pl.ds(0, n - 1)]
        pltpu.make_async_copy(left, left, out_sem.at[c]).wait()
        pltpu.make_async_copy(left, left, back_out_sem.at[c]).wait()
        return carry

    lax.fori_loop(0, coils, drain, 0)

    @pl.when(me < n - 1)
    def _():
        face_copy(0).wait_send()

    @pl.when(me > 0)
    def _():
        face_copy(1).wait_send()


def local(n, image, sensitivity, kernel):
    coils, _, _, ny, nz = sensitivity.shape
    gx, per, gz = kernel.shape
    nx, gy = n, n * per
    consts = [jnp.asarray(t) for t in tables(nx, ny, nz, gx, gy, gz)]
    whole = pl.BlockSpec(memory_space=pl.ANY)
    half = jnp.bfloat16
    return pl.pallas_call(
        functools.partial(body, n),
        out_shape=jax.ShapeDtypeStruct(image.shape, image.dtype),
        in_specs=[whole] * 9,
        out_specs=pl.BlockSpec(memory_space=pltpu.VMEM),
        scratch_shapes=[
            pltpu.VMEM((2, ny, nz), jnp.float32),
            pltpu.VMEM((coils, 2, ny, nz), half),
            pltpu.VMEM((per, gx, gz), jnp.float32),
            *[pltpu.VMEM(t.shape, half) for t in consts],
            pltpu.VMEM((coils, n, per, 2, nz), half),
            pltpu.VMEM((coils, per, n, 2, nz), half),
            pltpu.VMEM((coils, per, n, 2, nz), half),
            pltpu.VMEM((coils, n, per, 2, nz), half),
            pltpu.VMEM((2, ny, nz), half),
            pltpu.VMEM((2, 2, ny, nz), half),
            pltpu.VMEM((2, ny, nz), jnp.float32),
            pltpu.SemaphoreType.DMA((8 + per,)),
            pltpu.SemaphoreType.DMA((coils,)),
            pltpu.SemaphoreType.DMA((coils,)),
            pltpu.SemaphoreType.DMA((coils,)),
            pltpu.SemaphoreType.DMA((coils,)),
            pltpu.SemaphoreType.DMA((2,)),
            pltpu.SemaphoreType.DMA((2,)),
        ],
        compiler_params=pltpu.CompilerParams(collective_id=0, has_side_effects=True),
        name="normal_operator",
    )(image, sensitivity, kernel, *consts)


def solution(mesh):
    return jax.shard_map(
        functools.partial(local, mesh.shape["slab"]),
        mesh=mesh,
        in_specs=(
            P(None, "slab", "scan", None),
            P("scan", None, "slab", None, None),
            P(None, "slab", None),
        ),
        out_specs=P(None, "slab", "scan", None),
        check_vma=False,
    )
```

time: 141 us -> 107 us (0.76); the launches traced: 139 us -> 107 us
  Pallas kernels: 0 us -> 105 us
  waiting for transfers between devices: 72.9 us -> 0 us
  starting transfers between devices: 48.2 us -> 0 us
  matrix products: 7.59 us -> 0 us
  local copies, waits for them, and re-layouts: 7.55 us -> 1.57 us
  other arithmetic: 2.58 us -> 0 us
    pallas_call x0 -> x1, Pallas kernels: none -> 105 us  [local(): pl.pallas_call(functools.partial(body, n), out_shape=jax.ShapeDtypeStruct...]
    all_to_all x2 -> x0, waiting for transfers between devices: 72.9 us -> none  [the longest x1 38.4 us: local(): lax.all_to_all(along_second, 'slab', split_axis=3, concat_axis=2, tiled=T...]
    all_to_all x2 -> x0, starting transfers between devices: 42.4 us -> none  [the longest x1 31 us: local(): lax.all_to_all(along_second, 'slab', split_axis=3, concat_axis=2, tiled=T...]
    dot_general x5 -> x0, matrix products: 7.59 us -> none  [apply_table(): jnp.einsum(pattern, matrix, values, preferred_element_type=jnp.float32)]
    ppermute x2 -> x0, starting transfers between devices: 5.82 us -> none  [the longest x1 3.57 us: with_halo(): lax.ppermute(tail, axis, [(i, (i + 1) % count) for i in range(ends)])]
    convert_element_type x2 -> x0, local copies, waits for them, and re-layouts: 3.56 us -> none  [the longest x1 1.88 us: local(): apply_table(forward_second, coil_images, 'pqkj,cqajb->cpakb')]
    another operation x7 -> x0, other arithmetic: 2.29 us -> none
  transfers between devices with their start and end apart: 4 -> 0, of which waited for: 2 -> 0; matrix products, arithmetic and copies ran while one was open for 2% -> 0% of each run, Pallas kernels for 0% -> 0%
where the time goes in v1:
time: 107 us
  Pallas kernels  105 us (98%)
  local copies, waits for them, and re-layouts  1.57 us (1%)
    pallas_call x1, Pallas kernels, local(): pl.pallas_call(functools.partial(body, n), out_shape=jax.ShapeDtypeStruct...  105 us

profile of v1, /device:TPU:33, one launch (start us, length us, event | category | flops | bytes accessed | tf_op | source)
XLA Modules:
  0.0 106.6 jit_solution(8585688930056556215)
XLA Ops:
  0.0 105.0 %normal_operator.1 = f32[2,1,128,128]{3,2,1,0:T(8,128)} custom-call(f32[2,1,128,128]{3,2,1,0:T(8,128)} %image_hbm.1, bf16[6,2,1,128,128]{4,3,2,1,0:T(8,128)(2,1)} %maps_hbm.1, f32[256,2,256]{2,1,0:T(2,128)} %kernel_hbm.1, bf16[512,256]{1,0:T(8,128)(2,1)} %constant.12.clone.refs_0_, bf16[512,256]{1,0:T(8,128)(2,1)} %constant.13.clone.refs_1_, ...), custom_call_target="tpu_custom_call" | custom-call | tf_op jit(solution)/shard_map/normal_operator/pallas_call | solution.py:235
  105.0 1.6 %copy.11 = f32[2,1,128,128]{3,2,1,0:T(8,128)} copy(f32[2,1,128,128]{3,2,1,0:T(8,128)} %normal_operator.1) | data formatting | bytes 262144

commit v2 on v1

--- a/solution.py
+++ b/solution.py
@@ -12,6 +12,7 @@
 
 MESH = pl.DeviceIdType.MESH
 smooth_weight = 0.1
+group = 3
 
 
 def factor(count_out, count_in, length, sign):
@@ -94,29 +95,29 @@
     lax.fori_loop(0, coils, spread, 0)
     pl.semaphore_wait(barrier, n - 1)
 
-    def send(c, d):
+    def send(g, d):
         pltpu.make_async_remote_copy(
-            lines.at[c, d],
-            spectra.at[c, :, me],
-            out_sem.at[c],
-            in_sem.at[c],
+            lines.at[pl.ds(g * group, group), d],
+            spectra.at[pl.ds(g * group, group), :, me],
+            out_sem.at[g],
+            in_sem.at[g],
             device_id={"slab": d},
             device_id_type=MESH,
         ).start()
 
-    def send_back(c, d):
+    def send_back(g, d):
         pltpu.make_async_remote_copy(
-            backs.at[c, :, d],
-            planes.at[c, me],
-            back_out_sem.at[c],
-            back_in_sem.at[c],
+            backs.at[pl.ds(g * group, group), :, d],
+            planes.at[pl.ds(g * group, group), me],
+            back_out_sem.at[g],
+            back_in_sem.at[g],
             device_id={"slab": d},
             device_id_type=MESH,
         ).start()
 
-    def each(act, c):
+    def each(act, g):
         def step(k, carry):
-            act(c, lax.rem(me + k, n))
+            act(g, lax.rem(me + k, n))
             return carry
 
         lax.fori_loop(1, n, step, 0)
@@ -139,17 +140,17 @@
     def _():
         face_copy(1).start()
 
-    def start(c, carry):
-        each(send, c)
-        return carry
-
-    lax.fori_loop(0, coils, start, 0)
+    groups = coils // group
+
+    def start(g, carry):
+        each(send, g)
+        return carry
+
+    lax.fori_loop(0, groups, start, 0)
     for load in loads[3:]:
         load.wait()
 
     def middle(c, carry):
-        arrived = spectra.at[c, :, pl.ds(0, n - 1)]
-        pltpu.make_async_copy(arrived, arrived, in_sem.at[c]).wait()
         for i in range(per):
             x = spectra.at[c, i].reshape(2 * n, nz)[...]
             along = dot(table[1][...], x).astype(jnp.bfloat16)
@@ -166,10 +167,16 @@
             first = dot(table[4][...], columns).astype(jnp.bfloat16)
             backs.at[c, i].reshape(2 * n, nz)[...] = first
         planes[c, me] = backs[c, :, me]
-        each(send_back, c)
-        return carry
-
-    lax.fori_loop(0, coils, middle, 0)
+        return carry
+
+    def turn(g, carry):
+        arrived = spectra.at[pl.ds(g * group, group), :, pl.ds(0, n - 1)]
+        pltpu.make_async_copy(arrived, arrived, in_sem.at[g]).wait()
+        lax.fori_loop(g * group, (g + 1) * group, middle, 0)
+        each(send_back, g)
+        return carry
+
+    lax.fori_loop(0, groups, turn, 0)
 
     @pl.when(me > 0)
     def _():
@@ -196,8 +203,6 @@
         total[p] = smooth_weight * (6.0 * plane - beside)
 
     def finish(c, carry):
-        arrived = planes.at[c, pl.ds(0, n - 1)]
-        pltpu.make_async_copy(arrived, arrived, back_in_sem.at[c]).wait()
         coil = dot(table[5][...], planes.at[c].reshape(n * per * 2, nz)[...])
         coil_real, coil_imaginary = coil[:ny], coil[ny:]
         real, imaginary = maps[c, 0].astype(jnp.float32), maps[c, 1].astype(jnp.float32)
@@ -205,16 +210,21 @@
         total[1] += real * coil_imaginary - imaginary * coil_real
         return carry
 
-    lax.fori_loop(0, coils, finish, 0)
+    def gather(g, carry):
+        arrived = planes.at[pl.ds(g * group, group), pl.ds(0, n - 1)]
+        pltpu.make_async_copy(arrived, arrived, back_in_sem.at[g]).wait()
+        return lax.fori_loop(g * group, (g + 1) * group, finish, carry)
+
+    lax.fori_loop(0, groups, gather, 0)
     out[:, 0] = total[...]
 
-    def drain(c, carry):
-        left = lines.at[c, pl.ds(0, n - 1)]
-        pltpu.make_async_copy(left, left, out_sem.at[c]).wait()
-        pltpu.make_async_copy(left, left, back_out_sem.at[c]).wait()
-        return carry
-
-    lax.fori_loop(0, coils, drain, 0)
+    def drain(g, carry):
+        left = lines.at[pl.ds(g * group, group), pl.ds(0, n - 1)]
+        pltpu.make_async_copy(left, left, out_sem.at[g]).wait()
+        pltpu.make_async_copy(left, left, back_out_sem.at[g]).wait()
+        return carry
+
+    lax.fori_loop(0, groups, drain, 0)
 
     @pl.when(me < n - 1)
     def _():
@@ -250,10 +260,10 @@
             pltpu.VMEM((2, 2, ny, nz), half),
             pltpu.VMEM((2, ny, nz), jnp.float32),
             pltpu.SemaphoreType.DMA((8 + per,)),
-            pltpu.SemaphoreType.DMA((coils,)),
-            pltpu.SemaphoreType.DMA((coils,)),
-            pltpu.SemaphoreType.DMA((coils,)),
-            pltpu.SemaphoreType.DMA((coils,)),
+            pltpu.SemaphoreType.DMA((coils // group,)),
+            pltpu.SemaphoreType.DMA((coils // group,)),
+            pltpu.SemaphoreType.DMA((coils // group,)),
+            pltpu.SemaphoreType.DMA((coils // group,)),
             pltpu.SemaphoreType.DMA((2,)),
             pltpu.SemaphoreType.DMA((2,)),
         ],

time: 107 us -> 104 us (0.972)
  Pallas kernels: 105 us -> 102 us
    pallas_call x1, Pallas kernels: 105 us -> 102 us  [local(): pl.pallas_call(functools.partial(body, n), out_shape=jax.ShapeDtypeStruct...]
where the time goes in v2:
time: 104 us; the launch traced here: 103 us
  Pallas kernels  102 us (98%)
  local copies, waits for them, and re-layouts  1.57 us (2%)
    pallas_call x1, Pallas kernels, local(): pl.pallas_call(functools.partial(body, n), out_shape=jax.ShapeDtypeStruct...  102 us

profile of v2, /device:TPU:33, one launch (start us, length us, event | category | flops | bytes accessed | tf_op | source)
XLA Modules:
  0.0 103.4 jit_solution(2616771991444513831)
XLA Ops:
  0.0 101.8 %normal_operator.1 = f32[2,1,128,128]{3,2,1,0:T(8,128)} custom-call(f32[2,1,128,128]{3,2,1,0:T(8,128)} %image_hbm.1, bf16[6,2,1,128,128]{4,3,2,1,0:T(8,128)(2,1)} %maps_hbm.1, f32[256,2,256]{2,1,0:T(2,128)} %kernel_hbm.1, bf16[512,256]{1,0:T(8,128)(2,1)} %constant.12.clone.refs_0_, bf16[512,256]{1,0:T(8,128)(2,1)} %constant.13.clone.refs_1_, ...), custom_call_target="tpu_custom_call" | custom-call | tf_op jit(solution)/shard_map/normal_operator/pallas_call | solution.py:245
  101.8 1.6 %copy.11 = f32[2,1,128,128]{3,2,1,0:T(8,128)} copy(f32[2,1,128,128]{3,2,1,0:T(8,128)} %normal_operator.1) | data formatting | bytes 262144

commit v3 on v2

--- a/solution.py
+++ b/solution.py
@@ -76,7 +76,7 @@
         )
         return carry
 
-    lax.fori_loop(1, n, greet, 0)
+    lax.fori_loop(1, n, greet, 0, unroll=4)
 
     for load in loads[:3]:
         load.wait()
@@ -120,7 +120,7 @@
             act(g, lax.rem(me + k, n))
             return carry
 
-        lax.fori_loop(1, n, step, 0)
+        lax.fori_loop(1, n, step, 0, unroll=4)
 
     def face_copy(side):
         return pltpu.make_async_remote_copy(

time: 104 us -> 103 us (level)
  no operation moved by 1% of the time
where the time goes in v3:
time: 103 us
  Pallas kernels  101 us (98%)
  local copies, waits for them, and re-layouts  1.57 us (2%)
    pallas_call x1, Pallas kernels, local(): pl.pallas_call(functools.partial(body, n), out_shape=jax.ShapeDtypeStruct...  101 us

profile of v3, /device:TPU:33, one launch (start us, length us, event | category | flops | bytes accessed | tf_op | source)
XLA Modules:
  0.0 103.0 jit_solution(6468579240497864089)
XLA Ops:
  0.0 101.5 %normal_operator.1 = f32[2,1,128,128]{3,2,1,0:T(8,128)} custom-call(f32[2,1,128,128]{3,2,1,0:T(8,128)} %image_hbm.1, bf16[6,2,1,128,128]{4,3,2,1,0:T(8,128)(2,1)} %maps_hbm.1, f32[256,2,256]{2,1,0:T(2,128)} %kernel_hbm.1, bf16[512,256]{1,0:T(8,128)(2,1)} %constant.12.clone.refs_0_, bf16[512,256]{1,0:T(8,128)(2,1)} %constant.13.clone.refs_1_, ...), custom_call_target="tpu_custom_call" | custom-call | tf_op jit(solution)/shard_map/normal_operator/pallas_call | solution.py:245
  101.5 1.6 %copy.11 = f32[2,1,128,128]{3,2,1,0:T(8,128)} copy(f32[2,1,128,128]{3,2,1,0:T(8,128)} %normal_operator.1) | data formatting | bytes 262144

commit v4 on v3

--- a/solution.py
+++ b/solution.py
@@ -12,7 +12,7 @@
 
 MESH = pl.DeviceIdType.MESH
 smooth_weight = 0.1
-group = 3
+group = 2
 
 
 def factor(count_out, count_in, length, sign):

time: 103 us -> 103 us (level)
  no operation moved by 1% of the time
where the time goes in v4:
time: 103 us
  Pallas kernels  101 us (98%)
  local copies, waits for them, and re-layouts  1.57 us (2%)
    pallas_call x1, Pallas kernels, local(): pl.pallas_call(functools.partial(body, n), out_shape=jax.ShapeDtypeStruct...  101 us

profile of v4, /device:TPU:33, one launch (start us, length us, event | category | flops | bytes accessed | tf_op | source)
XLA Modules:
  0.0 102.6 jit_solution(14744674704175735843)
XLA Ops:
  0.0 101.0 %normal_operator.1 = f32[2,1,128,128]{3,2,1,0:T(8,128)} custom-call(f32[2,1,128,128]{3,2,1,0:T(8,128)} %image_hbm.1, bf16[6,2,1,128,128]{4,3,2,1,0:T(8,128)(2,1)} %maps_hbm.1, f32[256,2,256]{2,1,0:T(2,128)} %kernel_hbm.1, bf16[512,256]{1,0:T(8,128)(2,1)} %constant.12.clone.refs_0_, bf16[512,256]{1,0:T(8,128)(2,1)} %constant.13.clone.refs_1_, ...), custom_call_target="tpu_custom_call" | custom-call | tf_op jit(solution)/shard_map/normal_operator/pallas_call | solution.py:245
  101.0 1.6 %copy.11 = f32[2,1,128,128]{3,2,1,0:T(8,128)} copy(f32[2,1,128,128]{3,2,1,0:T(8,128)} %normal_operator.1) | data formatting | bytes 262144
